TPU v7x, 32 devices: a whole 2x2x4 slice. The times are simulated.
32 devices in a mesh: ep: 4 (over y, x), fsdp: 8 (over z, core).
Axes of the slice: x: 2, y: 2, z: 4, core: 2. Of those that a mesh axis runs over, the one named last changes fastest.
Arguments:
- master_down: float32 [16, 6400, 4096], P('ep', None, 'fsdp'), may hold values from -0.109375 to 0.109375
- second_down: bfloat16 [16, 6400, 4096], P('ep', None, 'fsdp'), may hold values from -0.0390625 to 0.0390625
- router_weight: float32 [4096, 16], P('fsdp', 'ep'), may hold values from -0.09375 to 0.09375
- router_gain: float32 [4096], P('fsdp'), may hold values from 0.25 to 1.75
Outputs:
- final_down: bfloat16 [16, 6400, 4096], P('ep', 'fsdp')
- scale_down: float32 [16, 6400], P('ep', 'fsdp')
- serve_router: bfloat16 [4096, 16], replicated
All inputs are finite; a program needn't handle non-finite values. Where the computation divides by a largest or mean magnitude, that divisor is 1e-20 or more.
Results may differ from a plain program's by a relative error of at most 0.001.
Values may be sent and summed in bfloat16 or wider, within the bound.
A program may use at most 256 MiB of HBM per device.

v0:
```python
import functools

import jax
import jax.numpy as jnp
from jax import lax
from jax.experimental import pallas as pl
from jax.experimental.pallas import tpu as pltpu
from jax.sharding import PartitionSpec as P

MESH = pl.DeviceIdType.MESH
LANES = 128
SLOTS = 3


def partner(me, step, count):
    result, bit = 0, 1
    while bit < count:
        mine, theirs = (me // bit) % 2, (step // bit) % 2
        result = result + bit * (mine + theirs - 2 * mine * theirs)
        bit *= 2
    return result


def kernel(sizes, master, second, router, gain, final, scale_out, router_out,
           wide, change, narrow, local_max, peer_max, scales, inverse, parts,
           load_sem, rs_send, rs_recv, ag_send, ag_recv, send_sem, recv_sem,
           ep_send, ep_recv, row_send, row_recv):
    experts, rows, columns, blocks, n_ep, n_fsdp = sizes
    me, group = lax.axis_index("fsdp"), lax.axis_index("ep")
    lead = min(3, experts)
    passes = [("max", expert) for expert in range(lead)]
    for expert in range(experts):
        passes.append(("scale", expert))
        if lead + expert < experts:
            passes.append(("max", lead + expert))

    def loads(t, expert, step):
        slot, owner = t % SLOTS, partner(me, step, n_fsdp)
        span = pl.ds(pl.multiple_of(owner * rows, 8), rows)
        return (
            pltpu.make_async_copy(
                master.at[expert, span, :], wide.at[slot, pl.ds(0, rows), :], load_sem.at[0, slot]),
            pltpu.make_async_copy(
                second.at[expert, span, :], change.at[slot, pl.ds(0, rows), :], load_sem.at[1, slot]),
        )

    def start_loads(t, expert, step):
        for copy in loads(t, expert, step):
            copy.start()

    def wait_loads(t, expert, step):
        for copy in loads(t, expert, step):
            copy.wait()

    def load_ahead(index, step):
        expert, ahead = passes[index][1], step + SLOTS
        if index + 1 < len(passes):
            later = passes[index + 1][1]
            start_loads(index * n_fsdp + ahead, expert + (later - expert) * (ahead // n_fsdp), ahead % n_fsdp)
        else:
            @pl.when(ahead < n_fsdp)
            def _():
                start_loads(index * n_fsdp + ahead, expert, ahead)

    def to_fsdp(source, target, send, recv, owner):
        return pltpu.make_async_remote_copy(
            src_ref=source, dst_ref=target, send_sem=send, recv_sem=recv,
            device_id={"fsdp": owner}, device_id_type=MESH)

    def max_copy(expert, step):
        owner = partner(me, step, n_fsdp)
        return to_fsdp(local_max.at[owner, expert], peer_max.at[step, expert],
                       rs_send.at[expert, step], rs_recv.at[expert, step], owner)

    def scale_copy(expert, step):
        owner = partner(me, step, n_fsdp)
        return to_fsdp(scales.at[me, expert], scales.at[me, expert],
                       ag_send.at[expert, step], ag_recv.at[expert, step], owner)

    def piece_copy(expert, step):
        owner = partner(me, step, n_fsdp)
        return to_fsdp(narrow.at[expert, owner, pl.ds(0, rows), :],
                       final.at[expert, :, pl.ds(pl.multiple_of(me * columns, LANES), columns)],
                       send_sem.at[expert, step], recv_sem.at[expert, step], owner)

    def own_copy(expert):
        return pltpu.make_async_copy(
            narrow.at[expert, me, pl.ds(0, rows), :],
            final.at[expert, :, pl.ds(pl.multiple_of(me * columns, LANES), columns)],
            send_sem.at[expert, 0])

    def column_copy(step):
        return pltpu.make_async_remote_copy(
            src_ref=parts.at[me, group], dst_ref=parts.at[me, group],
            send_sem=ep_send.at[step], recv_sem=ep_recv.at[step],
            device_id={"ep": partner(group, step, n_ep)}, device_id_type=MESH)

    def row_copy(step):
        return to_fsdp(parts.at[me], parts.at[me], row_send.at[step], row_recv.at[step],
                       partner(me, step, n_fsdp))

    def over(start, stop, body):
        def run(step, carry):
            body(step)
            return carry
        lax.fori_loop(start, stop, run, 0)

    for t in range(SLOTS):
        start_loads(t, 0, t)
    parts[me, group] = (router[...] * gain[...]).astype(jnp.bfloat16)
    local_max[...] = jnp.zeros_like(local_max)
    if rows < blocks * LANES:
        for slot in range(SLOTS):
            wide[slot, rows:, :] = jnp.zeros((blocks * LANES - rows, columns), jnp.float32)
            change[slot, rows:, :] = jnp.zeros((blocks * LANES - rows, columns), jnp.bfloat16)

    barrier = pltpu.get_barrier_semaphore()
    for step in range(1, n_fsdp):
        pl.semaphore_signal(barrier, inc=1, device_id={"fsdp": partner(me, step, n_fsdp)}, device_id_type=MESH)
    for step in range(1, n_ep):
        pl.semaphore_signal(barrier, inc=1, device_id={"ep": partner(group, step, n_ep)}, device_id_type=MESH)
    pl.semaphore_wait(barrier, n_fsdp + n_ep - 2)
    over(1, n_ep, lambda step: column_copy(step).start())

    def merged(slot, block):
        span = pl.ds(block * LANES, LANES)
        return wide[slot, span, :] + change[slot, span, :].astype(jnp.float32)

    def share_scales(expert):
        over(1, n_fsdp, lambda step: max_copy(expert, step).wait_recv())
        top = local_max[me, expert]
        for step in range(1, n_fsdp):
            top = jnp.maximum(top, peer_max[step, expert])
        scales[me, expert] = top
        over(1, n_fsdp, lambda step: scale_copy(expert, step).start())

    def find_max(index, expert, step):
        t = index * n_fsdp + step
        wait_loads(t, expert, step)
        owner, slot = partner(me, step, n_fsdp), t % SLOTS
        for block in range(blocks):
            sizes_of = jnp.abs(merged(slot, block))
            top = sizes_of[:, :LANES]
            for first in range(LANES, columns, LANES):
                top = jnp.maximum(top, sizes_of[:, first:first + LANES])
            local_max[owner, expert, pl.ds(block, 1), :] = jnp.max(top.T, axis=0, keepdims=True)
        load_ahead(index, step)

    def scale_piece(index, expert, step):
        t = index * n_fsdp + step
        wait_loads(t, expert, step)
        owner, slot = partner(me, step, n_fsdp), t % SLOTS
        for block in range(blocks):
            row = inverse[owner, pl.ds(block, 1), :]
            factor = jnp.broadcast_to(row, (LANES, LANES)).T
            whole = merged(slot, block)
            for first in range(0, columns, LANES):
                narrow[expert, owner, pl.ds(block * LANES, LANES), first:first + LANES] = (
                    whole[:, first:first + LANES] * factor).astype(jnp.bfloat16)
        load_ahead(index, step)

        @pl.when(step == 0)
        def _():
            own_copy(expert).start()

        @pl.when(step > 0)
        def _():
            piece_copy(expert, step).start()

    for index, (kind, expert) in enumerate(passes):
        if kind == "max":
            over(0, n_fsdp, functools.partial(find_max, index, expert))
            if expert:
                share_scales(expert - 1)
            over(1, n_fsdp, lambda step: max_copy(expert, step).start())
            if expert == 0:
                over(1, n_ep, lambda step: column_copy(step).wait())
                over(1, n_fsdp, lambda step: row_copy(step).start())
        else:
            if expert == experts - lead + 1 or experts == lead == expert + 1:
                share_scales(experts - 1)
            over(1, n_fsdp, lambda step: scale_copy(expert, step).wait_recv())
            inverse[...] = 1.0 / scales[:, expert]
            over(0, n_fsdp, functools.partial(scale_piece, index, expert))

    scale_out[...] = scales[me]
    over(1, n_fsdp, lambda step: row_copy(step).wait())
    router_out[...] = parts[...]
    for expert in range(experts):
        own_copy(expert).wait()
        over(1, n_fsdp, lambda step: max_copy(expert, step).wait_send())
        over(1, n_fsdp, lambda step: scale_copy(expert, step).wait_send())
        over(1, n_fsdp, lambda step: piece_copy(expert, step).wait())


def solution(mesh):
    n_ep, n_fsdp = mesh.shape["ep"], mesh.shape["fsdp"]

    def on_device(master_down, second_down, router_weight, router_gain):
        experts, all_rows, columns = master_down.shape
        rows = all_rows // n_fsdp
        blocks = -(-rows // LANES)
        held = -(-blocks // 8) * 8
        depth, width = router_weight.shape
        dma = pltpu.SemaphoreType.DMA
        vmem, hbm = pl.BlockSpec(memory_space=pltpu.VMEM), pl.BlockSpec(memory_space=pl.ANY)
        final_down, scales, parts = pl.pallas_call(
            functools.partial(kernel, (experts, rows, columns, blocks, n_ep, n_fsdp)),
            out_shape=(
                jax.ShapeDtypeStruct((experts, rows, columns * n_fsdp), jnp.bfloat16),
                jax.ShapeDtypeStruct((experts, held, LANES), jnp.float32),
                jax.ShapeDtypeStruct((n_fsdp, n_ep, width, depth), jnp.bfloat16),
            ),
            in_specs=[hbm, hbm, vmem, vmem],
            out_specs=(hbm, vmem, vmem),
            scratch_shapes=[
                pltpu.VMEM((SLOTS, blocks * LANES, columns), jnp.float32),
                pltpu.VMEM((SLOTS, blocks * LANES, columns), jnp.bfloat16),
                pltpu.VMEM((experts, n_fsdp, blocks * LANES, columns), jnp.bfloat16),
                pltpu.VMEM((n_fsdp, experts, held, LANES), jnp.float32),
                pltpu.VMEM((n_fsdp, experts, held, LANES), jnp.float32),
                pltpu.VMEM((n_fsdp, experts, held, LANES), jnp.float32),
                pltpu.VMEM((n_fsdp, held, LANES), jnp.float32),
                pltpu.VMEM((n_fsdp, n_ep, width, depth), jnp.bfloat16),
                dma((2, SLOTS)),
                dma((experts, n_fsdp)), dma((experts, n_fsdp)),
                dma((experts, n_fsdp)), dma((experts, n_fsdp)),
                dma((experts, n_fsdp)), dma((experts, n_fsdp)),
                dma((n_ep,)), dma((n_ep,)), dma((n_fsdp,)), dma((n_fsdp,)),
            ],
            compiler_params=pltpu.CompilerParams(
                collective_id=0, has_side_effects=True, vmem_limit_bytes=60 * 1024 * 1024),
        )(master_down, second_down, router_weight.T, router_gain[None, :])
        scale_down = scales.reshape(experts, held * LANES)[:, :rows]
        serve_router = parts.transpose(0, 3, 1, 2).reshape(n_fsdp * depth, n_ep * width)
        return final_down, scale_down, serve_router

    placed = (P("ep", None, "fsdp"), P("ep", None, "fsdp"), P("fsdp", "ep"), P("fsdp"))
    return jax.shard_map(
        on_device,
        mesh=mesh,
        in_specs=placed,
        out_specs=(P("ep", "fsdp", None), P("ep", "fsdp"), P()),
        check_vma=False,
    )
```

profile of v0, /device:TPU:9, one launch (start us, length us, event | category | flops | bytes accessed | tf_op | source)
XLA Modules:
  0.0 614.0 jit_solution(15997345063815766350)
XLA Ops:
  0.6 592.4 %shard_map.67 = (bf16[4,800,4096]{2,1,0:T(8,128)(2,1)}, f32[4,8,128]{2,1,0:T(8,128)}, bf16[8,4,4,512]{3,2,1,0:T(4,128)(2,1)}) custom-call(f32[4,6400,512]{2,1,0:T(8,128)} %master.1, bf16[4,6400,512]{2,1,0:T(8,128)(2,1)} %second.1, f32[4,512]{1,0:T(4,128)} %bitcast.17, f32[1,512]{1,0:T(1,128)} %bitcast.18), custom_call_target="tpu_custom_call" | custom-call | tf_op jit(solution)/shard_map/pallas_call | solution.py:207
  593.1 0.7 copy.11
  593.8 0.6 slice.4
  594.4 1.0 copy.7
  595.4 0.7 copy.9
  596.1 17.9 %copy.13 = bf16[4,800,4096]{2,1,0:T(8,128)(2,1)} copy(bf16[4,800,4096]{2,1,0:T(8,128)(2,1)} %get-tuple-element.12) | data formatting | bytes 52428800
where the time goes:
time: 614 us
  Pallas kernels  592 us (96%)
  local copies, waits for them, and re-layouts  20.9 us (3%)
    pallas_call x1, Pallas kernels, on_device(): pl.pallas_call(functools.partial(kernel, (experts, rows, columns, blocks,...  592 us
    unnamed x3, local copies, waits for them, and re-layouts  19.4 us

commit v1 on v0

v1 whole, which is shorter than its diff:
```python
import functools

import jax
import jax.numpy as jnp
from jax import lax
from jax.experimental import pallas as pl
from jax.experimental.pallas import tpu as pltpu
from jax.sharding import PartitionSpec as P

MESH = pl.DeviceIdType.MESH
LANES = 128
SLOTS = 3


def partner(me, step, count):
    result, bit = 0, 1
    while bit < count:
        mine, theirs = (me // bit) % 2, (step // bit) % 2
        result = result + bit * (mine + theirs - 2 * mine * theirs)
        bit *= 2
    return result


def over(start, stop, body):
    def run(step, carry):
        body(step)
        return carry
    lax.fori_loop(start, stop, run, 0)


def exchange(sizes, master, second, router, gain, final, scales_out, parts,
             wide, change, head_wide, head_change, narrow, local_max, peer_max, scales, inverse,
             head_max, head_peer, head_inverse,
             load_sem, head_load, rs_send, rs_recv, ag_send, ag_recv, send_sem, recv_sem,
             top_send, top_recv, head_send, head_recv, ep_send, ep_recv, row_send, row_recv):
    experts, rows, columns, blocks, n_ep, n_fsdp = sizes
    me, group = lax.axis_index("fsdp"), lax.axis_index("ep")
    last = rows - (blocks - 1) * LANES
    half = n_fsdp // 2
    lead = min(3, experts)
    passes = [("max", expert) for expert in range(lead)]
    for expert in range(experts):
        passes.append(("scale", expert))
        if lead + expert < experts:
            passes.append(("max", lead + expert))
    turns = [half if kind == "scale" and expert == 0 else 0 for kind, expert in passes]
    mine = pl.ds(pl.multiple_of(me * columns, LANES), columns)

    def rows_of(block):
        return LANES if block < blocks - 1 else last

    def loads(t, expert, step):
        slot, owner = t % SLOTS, partner(me, step, n_fsdp)
        span = pl.ds(pl.multiple_of(owner * rows, 8), rows)
        return (
            pltpu.make_async_copy(
                master.at[expert, span, :], wide.at[slot, pl.ds(0, rows), :], load_sem.at[0, slot]),
            pltpu.make_async_copy(
                second.at[expert, span, :], change.at[slot, pl.ds(0, rows), :], load_sem.at[1, slot]),
        )

    def start_loads(t, expert, step):
        for copy in loads(t, expert, step):
            copy.start()

    def wait_loads(t, expert, step):
        for copy in loads(t, expert, step):
            copy.wait()

    def load_ahead(index, turn):
        expert, ahead = passes[index][1], turn + SLOTS
        if index + 1 < len(passes):
            later = passes[index + 1][1]
            over_end = ahead // n_fsdp
            shift = turns[index] + (turns[index + 1] - turns[index]) * over_end
            start_loads(index * n_fsdp + ahead, expert + (later - expert) * over_end, (ahead + shift) % n_fsdp)
        else:
            @pl.when(ahead < n_fsdp)
            def _():
                start_loads(index * n_fsdp + ahead, expert, (ahead + turns[index]) % n_fsdp)

    def head_loads(step):
        owner = partner(me, step, n_fsdp)
        span = pl.ds(pl.multiple_of(owner * rows, 8), LANES)
        return (
            pltpu.make_async_copy(master.at[0, span, :], head_wide.at[step], head_load.at[0, step]),
            pltpu.make_async_copy(second.at[0, span, :], head_change.at[step], head_load.at[1, step]),
        )

    def to_fsdp(source, target, send, recv, owner):
        return pltpu.make_async_remote_copy(
            src_ref=source, dst_ref=target, send_sem=send, recv_sem=recv,
            device_id={"fsdp": owner}, device_id_type=MESH)

    def top_copy(step):
        return to_fsdp(head_max, head_peer.at[step], top_send.at[step], top_recv.at[step],
                       partner(me, step, n_fsdp))

    def max_copy(expert, step):
        owner = partner(me, step, n_fsdp)
        return to_fsdp(local_max.at[owner, expert], peer_max.at[step, expert],
                       rs_send.at[expert, step], rs_recv.at[expert, step], owner)

    def scale_copy(expert, step):
        owner = partner(me, step, n_fsdp)
        return to_fsdp(scales.at[me, expert], scales.at[me, expert],
                       ag_send.at[expert, step], ag_recv.at[expert, step], owner)

    def head_copy(step):
        return to_fsdp(narrow.at[0, step - 1, pl.ds(0, LANES), :], final.at[0, pl.ds(0, LANES), mine],
                       head_send.at[step], head_recv.at[step], partner(me, step, n_fsdp))

    def piece_copy(expert, step):
        first = LANES if expert == 0 else 0
        span = pl.ds(first, rows - first)
        return to_fsdp(narrow.at[expert, step - 1, span, :], final.at[expert, span, mine],
                       send_sem.at[expert, step], recv_sem.at[expert, step], partner(me, step, n_fsdp))

    def row_copy(step):
        return to_fsdp(parts.at[me, group], parts.at[me, group], row_send.at[step], row_recv.at[step],
                       partner(me, step, n_fsdp))

    def column_copy(step):
        return pltpu.make_async_remote_copy(
            src_ref=parts.at[:, group], dst_ref=parts.at[:, group],
            send_sem=ep_send.at[step], recv_sem=ep_recv.at[step],
            device_id={"ep": partner(group, step, n_ep)}, device_id_type=MESH)

    for step in range(n_fsdp):
        for copy in head_loads(step):
            copy.start()
    for t in range(SLOTS):
        start_loads(t, 0, t)
    barrier = pltpu.get_barrier_semaphore()
    for step in range(1, n_fsdp):
        pl.semaphore_signal(barrier, inc=1, device_id={"fsdp": partner(me, step, n_fsdp)}, device_id_type=MESH)
    for step in range(1, n_ep):
        pl.semaphore_signal(barrier, inc=1, device_id={"ep": partner(group, step, n_ep)}, device_id_type=MESH)
    parts[me, group] = (router[...] * gain[...]).astype(jnp.bfloat16)
    local_max[...] = jnp.zeros_like(local_max)
    if last < LANES:
        for slot in range(SLOTS):
            wide[slot, rows:, :] = jnp.zeros((LANES - last, columns), jnp.float32)
            change[slot, rows:, :] = jnp.zeros((LANES - last, columns), jnp.bfloat16)

    def tops(whole):
        entries = jnp.abs(whole)
        top = entries[:, :LANES]
        for first in range(LANES, columns, LANES):
            top = jnp.maximum(top, entries[:, first:first + LANES])
        return jnp.max(top.T, axis=0, keepdims=True)

    def find_head(step):
        for copy in head_loads(step):
            copy.wait()
        whole = head_wide[step] + head_change[step].astype(jnp.float32)
        head_max[pl.ds(partner(me, step, n_fsdp), 1), :] = tops(whole)

    over(0, n_fsdp, find_head)
    pl.semaphore_wait(barrier, n_fsdp + n_ep - 2)
    over(1, n_fsdp, lambda step: top_copy(step).start())
    over(1, n_fsdp, lambda step: row_copy(step).start())

    def merged(slot, block, count):
        span = pl.ds(block * LANES, count)
        return wide[slot, span, :] + change[slot, span, :].astype(jnp.float32)

    def find_max(index, expert, turn):
        t = index * n_fsdp + turn
        wait_loads(t, expert, turn)
        owner, slot = partner(me, turn, n_fsdp), t % SLOTS
        for block in range(1 if expert == 0 else 0, blocks):
            local_max[owner, expert, pl.ds(block, 1), :] = tops(merged(slot, block, LANES))
        load_ahead(index, turn)

    def share_scales(expert):
        over(1, n_fsdp, lambda step: max_copy(expert, step).wait_recv())
        top = local_max[me, expert]
        for step in range(1, n_fsdp):
            top = jnp.maximum(top, peer_max[step, expert])
        scales[me, expert] = top
        if expert == 0:
            scales[me, 0, pl.ds(0, 1), :] = head_max[pl.ds(me, 1), :]
        over(1, n_fsdp, lambda step: scale_copy(expert, step).start())

    def spread(row):
        return jnp.broadcast_to(row, (LANES, LANES)).T

    def scale_block(whole, row, count, expert, block, step):
        factor = spread(row)[:count]
        span = pl.ds(block * LANES, count)
        for first in range(0, columns, LANES):
            part = (whole[:, first:first + LANES] * factor).astype(jnp.bfloat16)
            if step is None:
                final[expert, span, pl.ds(pl.multiple_of(me * columns + first, LANES), LANES)] = part
            else:
                narrow[expert, step - 1, span, first:first + LANES] = part

    def scale_head(step):
        source = 0 if step is None else step
        whole = head_wide[source] + head_change[source].astype(jnp.float32)
        row = head_inverse[pl.ds(partner(me, source, n_fsdp), 1), :]
        scale_block(whole, row, LANES, 0, 0, step)
        if step is not None:
            head_copy(step).start()

    def scale_piece(index, expert, own, turn):
        t = index * n_fsdp + turn
        step = (turn + turns[index]) % n_fsdp
        wait_loads(t, expert, step)
        owner, slot = partner(me, step, n_fsdp), t % SLOTS
        for block in range(1 if expert == 0 else 0, blocks):
            count = rows_of(block)
            scale_block(merged(slot, block, count), inverse[owner, pl.ds(block, 1), :], count,
                        expert, block, None if own else step)
        load_ahead(index, turn)
        if not own:
            piece_copy(expert, step).start()

    for index, (kind, expert) in enumerate(passes):
        if kind == "max":
            if index == 0:
                over(0, half, functools.partial(find_max, index, expert))
                over(1, n_fsdp, lambda step: top_copy(step).wait())
                top = head_max[...]
                for step in range(1, n_fsdp):
                    top = jnp.maximum(top, head_peer[step])
                head_max[...] = top
                head_inverse[...] = 1.0 / top
                over(half, half + half // 2, scale_head)
                over(half, n_fsdp, functools.partial(find_max, index, expert))
            else:
                over(0, n_fsdp, functools.partial(find_max, index, expert))
                share_scales(expert - 1)
            over(1, n_fsdp, lambda step: max_copy(expert, step).start())
            if expert == 0:
                over(half + half // 2, n_fsdp - 1, scale_head)
                if lead == 1:
                    share_scales(0)
            if expert == min(1, lead - 1):
                over(n_fsdp - 1, n_fsdp, scale_head)
                over(1, half, scale_head)
                scale_head(None)
                over(1, n_fsdp, lambda step: row_copy(step).wait())
                over(1, n_ep, lambda step: column_copy(step).start())
        else:
            if lead > 1 and expert == experts - lead + 1:
                share_scales(experts - 1)
            over(1, n_fsdp, lambda step: scale_copy(expert, step).wait_recv())
            inverse[...] = 1.0 / scales[:, expert]
            zero = (n_fsdp - turns[index]) % n_fsdp
            over(0, zero, functools.partial(scale_piece, index, expert, False))
            scale_piece(index, expert, True, zero)
            over(zero + 1, n_fsdp, functools.partial(scale_piece, index, expert, False))

    scales_out[...] = scales[me]
    over(1, n_ep, lambda step: column_copy(step).wait())
    over(1, n_fsdp, lambda step: head_copy(step).wait())
    for expert in range(experts):
        over(1, n_fsdp, lambda step: max_copy(expert, step).wait_send())
        over(1, n_fsdp, lambda step: scale_copy(expert, step).wait_send())
        over(1, n_fsdp, lambda step: piece_copy(expert, step).wait())


def write(sizes, pieces, scales, parts, final, scale_down, serve_router,
          scale_rows, router_rows, final_sem, small_sem):
    experts, rows, blocks, n_ep, n_fsdp, depth = sizes
    copies = [pltpu.make_async_copy(pieces.at[expert], final.at[expert], final_sem.at[expert])
              for expert in range(experts)]
    for copy in copies:
        copy.start()
    for block in range(blocks):
        count = min(LANES, rows - block * LANES)
        scale_rows[:, pl.ds(block * LANES, count)] = scales[:, block, :count]
    for place in range(n_fsdp):
        taken = [parts[place, group].astype(jnp.float32) for group in range(n_ep)]
        router_rows[:, place * depth:(place + 1) * depth] = (
            jnp.concatenate(taken, axis=0).astype(jnp.bfloat16))
    copies.append(pltpu.make_async_copy(scale_rows, scale_down, small_sem.at[0]))
    copies.append(pltpu.make_async_copy(router_rows, serve_router, small_sem.at[1]))
    for copy in copies[experts:]:
        copy.start()
    for copy in copies:
        copy.wait()


def solution(mesh):
    n_ep, n_fsdp = mesh.shape["ep"], mesh.shape["fsdp"]

    def on_device(master_down, second_down, router_weight, router_gain):
        experts, all_rows, columns = master_down.shape
        rows = all_rows // n_fsdp
        blocks = -(-rows // LANES)
        held = -(-blocks // 8) * 8
        depth, width = router_weight.shape
        dma = pltpu.SemaphoreType.DMA
        vmem, hbm = pl.BlockSpec(memory_space=pltpu.VMEM), pl.BlockSpec(memory_space=pl.ANY)
        pieces, scales, parts = pl.pallas_call(
            functools.partial(exchange, (experts, rows, columns, blocks, n_ep, n_fsdp)),
            out_shape=(
                pltpu.VMEM((experts, rows, columns * n_fsdp), jnp.bfloat16),
                pltpu.VMEM((experts, held, LANES), jnp.float32),
                pltpu.VMEM((n_fsdp, n_ep, width, depth), jnp.bfloat16),
            ),
            in_specs=[hbm, hbm, vmem, vmem],
            out_specs=(vmem, vmem, vmem),
            scratch_shapes=[
                pltpu.VMEM((SLOTS, blocks * LANES, columns), jnp.float32),
                pltpu.VMEM((SLOTS, blocks * LANES, columns), jnp.bfloat16),
                pltpu.VMEM((n_fsdp, LANES, columns), jnp.float32),
                pltpu.VMEM((n_fsdp, LANES, columns), jnp.bfloat16),
                pltpu.VMEM((experts, n_fsdp - 1, rows, columns), jnp.bfloat16),
                pltpu.VMEM((n_fsdp, experts, held, LANES), jnp.float32),
                pltpu.VMEM((n_fsdp, experts, held, LANES), jnp.float32),
                pltpu.VMEM((n_fsdp, experts, held, LANES), jnp.float32),
                pltpu.VMEM((n_fsdp, held, LANES), jnp.float32),
                pltpu.VMEM((n_fsdp, LANES), jnp.float32),
                pltpu.VMEM((n_fsdp, n_fsdp, LANES), jnp.float32),
                pltpu.VMEM((n_fsdp, LANES), jnp.float32),
                dma((2, SLOTS)), dma((2, n_fsdp)),
                dma((experts, n_fsdp)), dma((experts, n_fsdp)),
                dma((experts, n_fsdp)), dma((experts, n_fsdp)),
                dma((experts, n_fsdp)), dma((experts, n_fsdp)),
                dma((n_fsdp,)), dma((n_fsdp,)), dma((n_fsdp,)), dma((n_fsdp,)),
                dma((n_ep,)), dma((n_ep,)), dma((n_fsdp,)), dma((n_fsdp,)),
            ],
            compiler_params=pltpu.CompilerParams(
                collective_id=0, has_side_effects=True, vmem_limit_bytes=37 * 1024 * 1024),
        )(master_down, second_down, router_weight.T, router_gain[None, :])
        final_down, scale_down, serve_router = pl.pallas_call(
            functools.partial(write, (experts, rows, blocks, n_ep, n_fsdp, depth)),
            out_shape=(
                jax.ShapeDtypeStruct((experts, rows, columns * n_fsdp), jnp.bfloat16),
                jax.ShapeDtypeStruct((experts, rows), jnp.float32),
                jax.ShapeDtypeStruct((n_ep * width, n_fsdp * depth), jnp.bfloat16),
            ),
            in_specs=[vmem, vmem, vmem],
            out_specs=(hbm, hbm, hbm),
            scratch_shapes=[
                pltpu.VMEM((experts, rows), jnp.float32),
                pltpu.VMEM((n_ep * width, n_fsdp * depth), jnp.bfloat16),
                dma((experts,)), dma((2,)),
            ],
            compiler_params=pltpu.CompilerParams(vmem_limit_bytes=4 * 1024 * 1024),
        )(pieces, scales, parts)
        return final_down, scale_down, serve_router.T

    placed = (P("ep", None, "fsdp"), P("ep", None, "fsdp"), P("fsdp", "ep"), P("fsdp"))
    return jax.shard_map(
        on_device,
        mesh=mesh,
        in_specs=placed,
        out_specs=(P("ep", "fsdp", None), P("ep", "fsdp"), P()),
        check_vma=False,
    )
```

time: 614 us -> 591 us (0.963)
  local copies, waits for them, and re-layouts: 20.9 us -> 0 us
    unnamed x3 -> x0, local copies, waits for them, and re-layouts: 19.4 us -> none
    pallas_call x1 -> x2, Pallas kernels: 592 us -> 590 us  [the longest x1 581 us: on_device(): pl.pallas_call(functools.partial(exchange, (experts, rows, columns, block...]
where the time goes in v1:
time: 591 us; the launch traced here: 590 us
  Pallas kernels  590 us (100%)
    pallas_call x1, Pallas kernels, on_device(): pl.pallas_call(functools.partial(exchange, (experts, rows, columns, block...  581 us

profile of v1, /device:TPU:9, one launch (start us, length us, event | category | flops | bytes accessed | tf_op | source)
XLA Modules:
  0.0 590.4 jit_solution(13045809474176700714)
XLA Ops:
  0.6 580.8 %shard_map.67 = (bf16[4,800,4096]{2,1,0:T(8,128)(2,1)S(1)}, f32[4,8,128]{2,1,0:T(8,128)S(1)}, bf16[8,4,4,512]{3,2,1,0:T(4,128)(2,1)S(1)}) custom-call(f32[4,6400,512]{2,1,0:T(8,128)} %master.1, bf16[4,6400,512]{2,1,0:T(8,128)(2,1)} %second.1, f32[4,512]{1,0:T(4,128)} %bitcast.3, f32[1,512]{1,0:T(1,128)} %bitcast.4), custom_call_target="tpu_custom_call" | custom-call | tf_op jit(solution)/shard_map/pallas_call | solution.py:298
  581.4 8.9 %shard_map.68 = (bf16[4,800,4096]{2,1,0:T(8,128)(2,1)}, f32[4,800]{1,0:T(4,128)}, bf16[16,4096]{1,0:T(8,128)(2,1)}) custom-call(bf16[4,800,4096]{2,1,0:T(8,128)(2,1)S(1)} %get-tuple-element.9.pieces, f32[4,8,128]{2,1,0:T(8,128)S(1)} %get-tuple-element.10.scales, bf16[8,4,4,512]{3,2,1,0:T(4,128)(2,1)S(1)} %get-tuple-element.11.parts), custom_call_target="tpu_custom_call" | custom-call | tf_op jit(solution)/shard_map/pallas_call | solution.py:330

commit v2 on v1

--- a/solution.py
+++ b/solution.py
@@ -10,6 +10,7 @@
 MESH = pl.DeviceIdType.MESH
 LANES = 128
 SLOTS = 3
+LATE = 2
 
 
 def partner(me, step, count):
@@ -28,13 +29,23 @@
     lax.fori_loop(start, stop, run, 0)
 
 
-def exchange(sizes, master, second, router, gain, final, scales_out, parts,
+def first_late(experts):
+    return experts - min(LATE, experts - 1)
+
+
+def is_inner(me, n_fsdp):
+    quarter = n_fsdp // 4
+    return (me >= (2 * quarter - 2)) & (me < 2 * quarter + 2)
+
+
+def exchange(sizes, master, second, router, gain, final, scales_out, parts, late,
              wide, change, head_wide, head_change, narrow, local_max, peer_max, scales, inverse,
              head_max, head_peer, head_inverse,
              load_sem, head_load, rs_send, rs_recv, ag_send, ag_recv, send_sem, recv_sem,
-             top_send, top_recv, head_send, head_recv, ep_send, ep_recv, row_send, row_recv):
+             top_send, top_recv, head_send, head_recv, ep_send, ep_recv, row_send, row_recv, go):
     experts, rows, columns, blocks, n_ep, n_fsdp = sizes
     me, group = lax.axis_index("fsdp"), lax.axis_index("ep")
+    inner = is_inner(me, n_fsdp)
     last = rows - (blocks - 1) * LANES
     half = n_fsdp // 2
     lead = min(3, experts)
@@ -43,7 +54,9 @@
         passes.append(("scale", expert))
         if lead + expert < experts:
             passes.append(("max", lead + expert))
+    fresh = first_late(experts)
     turns = [half if kind == "scale" and expert == 0 else 0 for kind, expert in passes]
+    starts = [expert * (n_fsdp - 1) - 2 * max(0, expert - fresh) for expert in range(experts)]
     mine = pl.ds(pl.multiple_of(me * columns, LANES), columns)
 
     def rows_of(block):
@@ -107,13 +120,17 @@
                        ag_send.at[expert, step], ag_recv.at[expert, step], owner)
 
     def head_copy(step):
-        return to_fsdp(narrow.at[0, step - 1, pl.ds(0, LANES), :], final.at[0, pl.ds(0, LANES), mine],
+        return to_fsdp(narrow.at[step - 1, pl.ds(0, LANES), :], final.at[0, pl.ds(0, LANES), mine],
                        head_send.at[step], head_recv.at[step], partner(me, step, n_fsdp))
 
-    def piece_copy(expert, step):
+    def piece_copy(expert, step, held_back=False):
         first = LANES if expert == 0 else 0
         span = pl.ds(first, rows - first)
-        return to_fsdp(narrow.at[expert, step - 1, span, :], final.at[expert, span, mine],
+        if held_back:
+            source = late.at[expert - fresh, step - (n_fsdp - 2), span, :]
+        else:
+            source = narrow.at[starts[expert] + step - 1, span, :]
+        return to_fsdp(source, final.at[expert, span, mine],
                        send_sem.at[expert, step], recv_sem.at[expert, step], partner(me, step, n_fsdp))
 
     def row_copy(step):
@@ -186,36 +203,53 @@
     def spread(row):
         return jnp.broadcast_to(row, (LANES, LANES)).T
 
-    def scale_block(whole, row, count, expert, block, step):
+    def scale_block(whole, row, count, expert, block, store):
         factor = spread(row)[:count]
         span = pl.ds(block * LANES, count)
         for first in range(0, columns, LANES):
             part = (whole[:, first:first + LANES] * factor).astype(jnp.bfloat16)
-            if step is None:
+            if store is None:
                 final[expert, span, pl.ds(pl.multiple_of(me * columns + first, LANES), LANES)] = part
             else:
-                narrow[expert, step - 1, span, first:first + LANES] = part
+                store(span, first, part)
 
     def scale_head(step):
         source = 0 if step is None else step
         whole = head_wide[source] + head_change[source].astype(jnp.float32)
         row = head_inverse[pl.ds(partner(me, source, n_fsdp), 1), :]
-        scale_block(whole, row, LANES, 0, 0, step)
-        if step is not None:
-            head_copy(step).start()
-
-    def scale_piece(index, expert, own, turn):
+        if step is None:
+            scale_block(whole, row, LANES, 0, 0, None)
+            return
+
+        def store(span, first, part):
+            narrow[step - 1, span, first:first + LANES] = part
+
+        scale_block(whole, row, LANES, 0, 0, store)
+        head_copy(step).start()
+
+    def scale_piece(index, expert, kind, turn):
         t = index * n_fsdp + turn
+
+        def to_narrow(span, first, part):
+            narrow[starts[expert] + step - 1, span, first:first + LANES] = part
+
+        def to_late(span, first, part):
+            late[expert - fresh, step - (n_fsdp - 2), span, first:first + LANES] = part
+
         step = (turn + turns[index]) % n_fsdp
         wait_loads(t, expert, step)
         owner, slot = partner(me, step, n_fsdp), t % SLOTS
         for block in range(1 if expert == 0 else 0, blocks):
             count = rows_of(block)
             scale_block(merged(slot, block, count), inverse[owner, pl.ds(block, 1), :], count,
-                        expert, block, None if own else step)
+                        expert, block, {"own": None, "sent": to_narrow, "late": to_late}[kind])
         load_ahead(index, turn)
-        if not own:
+        if kind == "sent":
             piece_copy(expert, step).start()
+        elif kind == "late" and expert < experts - 1:
+            @pl.when(jnp.logical_not(inner))
+            def _():
+                piece_copy(expert, step, True).start()
 
     for index, (kind, expert) in enumerate(passes):
         if kind == "max":
@@ -249,9 +283,11 @@
             over(1, n_fsdp, lambda step: scale_copy(expert, step).wait_recv())
             inverse[...] = 1.0 / scales[:, expert]
             zero = (n_fsdp - turns[index]) % n_fsdp
-            over(0, zero, functools.partial(scale_piece, index, expert, False))
-            scale_piece(index, expert, True, zero)
-            over(zero + 1, n_fsdp, functools.partial(scale_piece, index, expert, False))
+            stop = n_fsdp - 2 if expert >= fresh else n_fsdp
+            over(0, zero, functools.partial(scale_piece, index, expert, "sent"))
+            scale_piece(index, expert, "own", zero)
+            over(zero + 1, stop, functools.partial(scale_piece, index, expert, "sent"))
+            over(stop, n_fsdp, functools.partial(scale_piece, index, expert, "late"))
 
     scales_out[...] = scales[me]
     over(1, n_ep, lambda step: column_copy(step).wait())
@@ -259,16 +295,75 @@
     for expert in range(experts):
         over(1, n_fsdp, lambda step: max_copy(expert, step).wait_send())
         over(1, n_fsdp, lambda step: scale_copy(expert, step).wait_send())
-        over(1, n_fsdp, lambda step: piece_copy(expert, step).wait())
+        over(1, n_fsdp if expert < fresh else n_fsdp - 2, lambda step: piece_copy(expert, step).wait())
+    if fresh < experts:
+        @pl.when(inner)
+        def _():
+            for step in range(2, n_fsdp - 2):
+                pl.semaphore_signal(go, inc=1, device_id={"fsdp": partner(me, step, n_fsdp)}, device_id_type=MESH)
+
+        @pl.when(jnp.logical_not(inner))
+        def _():
+            pl.semaphore_wait(go, 4)
+            over(n_fsdp - 2, n_fsdp, lambda step: piece_copy(experts - 1, step, True).start())
+            for expert in range(fresh, experts):
+                over(n_fsdp - 2, n_fsdp, lambda step: piece_copy(expert, step, True).wait())
+
+
+def exchange_late(sizes, late, written, tail, send_sem, recv_sem):
+    experts, rows, n_fsdp = sizes
+    me = lax.axis_index("fsdp")
+    fresh = first_late(experts)
+
+    @pl.when(is_inner(me, n_fsdp))
+    def _():
+        barrier = pltpu.get_barrier_semaphore()
+        copies = []
+        for side in range(2):
+            peer = {"fsdp": partner(me, n_fsdp - 2 + side, n_fsdp)}
+            pl.semaphore_signal(barrier, inc=1, device_id=peer, device_id_type=MESH)
+            for expert in range(fresh, experts):
+                piece = (expert - fresh, side)
+                copies.append(pltpu.make_async_remote_copy(
+                    src_ref=late.at[piece], dst_ref=tail.at[piece],
+                    send_sem=send_sem.at[expert - fresh, side], recv_sem=recv_sem.at[expert - fresh, side],
+                    device_id=peer, device_id_type=MESH))
+        pl.semaphore_wait(barrier, 2)
+        for copy in copies:
+            copy.start()
+        for copy in copies:
+            copy.wait()
+
+
+def write_late(sizes, final_in, tail, final, sem):
+    experts, rows, columns, n_fsdp = sizes
+    me = lax.axis_index("fsdp")
+    fresh = first_late(experts)
+
+    @pl.when(is_inner(me, n_fsdp))
+    def _():
+        copies = []
+        for expert in range(fresh, experts):
+            for side in range(2):
+                source = partner(me, n_fsdp - 2 + side, n_fsdp)
+                copies.append(pltpu.make_async_copy(
+                    tail.at[expert - fresh, side],
+                    final.at[expert, :, pl.ds(pl.multiple_of(source * columns, LANES), columns)],
+                    sem.at[expert - fresh, side]))
+        for copy in copies:
+            copy.start()
+        for copy in copies:
+            copy.wait()
 
 
 def write(sizes, pieces, scales, parts, final, scale_down, serve_router,
-          scale_rows, router_rows, final_sem, small_sem):
+          token, scale_rows, router_rows, final_sem, small_sem):
     experts, rows, blocks, n_ep, n_fsdp, depth = sizes
     copies = [pltpu.make_async_copy(pieces.at[expert], final.at[expert], final_sem.at[expert])
               for expert in range(experts)]
     for copy in copies:
         copy.start()
+    token[...] = jnp.zeros_like(token)
     for block in range(blocks):
         count = min(LANES, rows - block * LANES)
         scale_rows[:, pl.ds(block * LANES, count)] = scales[:, block, :count]
@@ -295,21 +390,23 @@
         depth, width = router_weight.shape
         dma = pltpu.SemaphoreType.DMA
         vmem, hbm = pl.BlockSpec(memory_space=pltpu.VMEM), pl.BlockSpec(memory_space=pl.ANY)
-        pieces, scales, parts = pl.pallas_call(
+        n_late = experts - first_late(experts)
+        pieces, scales, parts, late = pl.pallas_call(
             functools.partial(exchange, (experts, rows, columns, blocks, n_ep, n_fsdp)),
             out_shape=(
                 pltpu.VMEM((experts, rows, columns * n_fsdp), jnp.bfloat16),
                 pltpu.VMEM((experts, held, LANES), jnp.float32),
                 pltpu.VMEM((n_fsdp, n_ep, width, depth), jnp.bfloat16),
+                pltpu.VMEM((max(n_late, 1), 2, rows, columns), jnp.bfloat16),
             ),
             in_specs=[hbm, hbm, vmem, vmem],
-            out_specs=(vmem, vmem, vmem),
+            out_specs=(vmem, vmem, vmem, vmem),
             scratch_shapes=[
                 pltpu.VMEM((SLOTS, blocks * LANES, columns), jnp.float32),
                 pltpu.VMEM((SLOTS, blocks * LANES, columns), jnp.bfloat16),
                 pltpu.VMEM((n_fsdp, LANES, columns), jnp.float32),
                 pltpu.VMEM((n_fsdp, LANES, columns), jnp.bfloat16),
-                pltpu.VMEM((experts, n_fsdp - 1, rows, columns), jnp.bfloat16),
+                pltpu.VMEM((experts * (n_fsdp - 1) - 2 * n_late, rows, columns), jnp.bfloat16),
                 pltpu.VMEM((n_fsdp, experts, held, LANES), jnp.float32),
                 pltpu.VMEM((n_fsdp, experts, held, LANES), jnp.float32),
                 pltpu.VMEM((n_fsdp, experts, held, LANES), jnp.float32),
@@ -323,19 +420,21 @@
                 dma((experts, n_fsdp)), dma((experts, n_fsdp)),
                 dma((n_fsdp,)), dma((n_fsdp,)), dma((n_fsdp,)), dma((n_fsdp,)),
                 dma((n_ep,)), dma((n_ep,)), dma((n_fsdp,)), dma((n_fsdp,)),
+                pltpu.SemaphoreType.REGULAR,
             ],
             compiler_params=pltpu.CompilerParams(
-                collective_id=0, has_side_effects=True, vmem_limit_bytes=37 * 1024 * 1024),
+                collective_id=0, has_side_effects=True, vmem_limit_bytes=32560 * 1024),
         )(master_down, second_down, router_weight.T, router_gain[None, :])
-        final_down, scale_down, serve_router = pl.pallas_call(
+        final_down, scale_down, serve_router, token = pl.pallas_call(
             functools.partial(write, (experts, rows, blocks, n_ep, n_fsdp, depth)),
             out_shape=(
                 jax.ShapeDtypeStruct((experts, rows, columns * n_fsdp), jnp.bfloat16),
                 jax.ShapeDtypeStruct((experts, rows), jnp.float32),
                 jax.ShapeDtypeStruct((n_ep * width, n_fsdp * depth), jnp.bfloat16),
+                pltpu.VMEM((8, LANES), jnp.float32),
             ),
             in_specs=[vmem, vmem, vmem],
-            out_specs=(hbm, hbm, hbm),
+            out_specs=(hbm, hbm, hbm, vmem),
             scratch_shapes=[
                 pltpu.VMEM((experts, rows), jnp.float32),
                 pltpu.VMEM((n_ep * width, n_fsdp * depth), jnp.bfloat16),
@@ -343,6 +442,26 @@
             ],
             compiler_params=pltpu.CompilerParams(vmem_limit_bytes=4 * 1024 * 1024),
         )(pieces, scales, parts)
+        if not n_late:
+            return final_down, scale_down, serve_router.T
+        tail = pl.pallas_call(
+            functools.partial(exchange_late, (experts, rows, n_fsdp)),
+            out_shape=pltpu.VMEM((n_late, 2, rows, columns), jnp.bfloat16),
+            in_specs=[vmem, vmem],
+            out_specs=vmem,
+            scratch_shapes=[dma((n_late, 2)), dma((n_late, 2))],
+            compiler_params=pltpu.CompilerParams(
+                collective_id=1, has_side_effects=True, vmem_limit_bytes=1024 * 1024),
+        )(late, token)
+        final_down = pl.pallas_call(
+            functools.partial(write_late, (experts, rows, columns, n_fsdp)),
+            out_shape=jax.ShapeDtypeStruct((experts, rows, columns * n_fsdp), jnp.bfloat16),
+            in_specs=[hbm, vmem],
+            out_specs=hbm,
+            scratch_shapes=[dma((n_late, 2))],
+            input_output_aliases={0: 0},
+            compiler_params=pltpu.CompilerParams(vmem_limit_bytes=1024 * 1024),
+        )(final_down, tail)
         return final_down, scale_down, serve_router.T
 
     placed = (P("ep", None, "fsdp"), P("ep", None, "fsdp"), P("fsdp", "ep"), P("fsdp"))

time: 591 us -> 584 us (0.988)
  Pallas kernels: 590 us -> 583 us
    pallas_call x1, Pallas kernels: 581 us -> 474 us  [on_device(): pl.pallas_call(functools.partial(exchange, (experts, rows, columns, block...]
    pallas_call x0 -> x2, Pallas kernels: none -> 100 us  [the longest x1 98.6 us: on_device(): pl.pallas_call(functools.partial(exchange_late, (experts, rows, n_fsdp)),...]
where the time goes in v2:
time: 584 us
  Pallas kernels  583 us (100%)
    pallas_call x1, Pallas kernels, on_device(): pl.pallas_call(functools.partial(exchange, (experts, rows, columns, block...  474 us
    pallas_call x1, Pallas kernels, on_device(): pl.pallas_call(functools.partial(exchange_late, (experts, rows, n_fsdp)),...  98.6 us

profile of v2, /device:TPU:9, one launch (start us, length us, event | category | flops | bytes accessed | tf_op | source)
XLA Modules:
  0.0 583.8 jit_solution(16749236039275902875)
XLA Ops:
  0.6 473.8 %shard_map.67 = (bf16[4,800,4096]{2,1,0:T(8,128)(2,1)S(1)}, f32[4,8,128]{2,1,0:T(8,128)S(1)}, bf16[8,4,4,512]{3,2,1,0:T(4,128)(2,1)S(1)}, bf16[2,2,800,512]{3,2,1,0:T(8,128)(2,1)S(1)}) custom-call(f32[4,6400,512]{2,1,0:T(8,128)} %master.1, bf16[4,6400,512]{2,1,0:T(8,128)(2,1)} %second.1, f32[4,512]{1,0:T(4,128)} %bitcast.3, f32[1,512]{1,0:T(1,128)} %bitcast.4), custom_call_target="tpu_custom_call" | custom-call | tf_op jit(solution)/shard_map/pallas_call | solution.py:394
  474.5 8.9 %shard_map.68 = (bf16[4,800,4096]{2,1,0:T(8,128)(2,1)}, f32[4,800]{1,0:T(4,128)}, bf16[16,4096]{1,0:T(8,128)(2,1)}, f32[8,128]{1,0:T(8,128)S(1)}) custom-call(bf16[4,800,4096]{2,1,0:T(8,128)(2,1)S(1)} %get-tuple-element.11.pieces, f32[4,8,128]{2,1,0:T(8,128)S(1)} %get-tuple-element.12.scales, bf16[8,4,4,512]{3,2,1,0:T(4,128)(2,1)S(1)} %get-tuple-element.13.parts), custom_call_target="tpu_custom_call" | custom-call | tf_op jit(solution)/shard_map/pallas_call | solution.py:428
  483.4 98.6 %shard_map.69.tail = bf16[2,2,800,512]{3,2,1,0:T(8,128)(2,1)S(1)} custom-call(bf16[2,2,800,512]{3,2,1,0:T(8,128)(2,1)S(1)} %get-tuple-element.15.late, f32[8,128]{1,0:T(8,128)S(1)} %get-tuple-element.16.written), custom_call_target="tpu_custom_call" | custom-call | tf_op jit(solution)/shard_map/pallas_call | solution.py:447
  582.0 1.8 shard_map.70

commit v3 on v2

--- a/solution.py
+++ b/solution.py
@@ -10,7 +10,7 @@
 MESH = pl.DeviceIdType.MESH
 LANES = 128
 SLOTS = 3
-LATE = 2
+LATE = 1
 
 
 def partner(me, step, count):
@@ -39,13 +39,14 @@
 
 
 def exchange(sizes, master, second, router, gain, final, scales_out, parts, late,
-             wide, change, head_wide, head_change, narrow, local_max, peer_max, scales, inverse,
+             wide, change, head_wide, head_change, narrow, local_max, pair_max, peer_max, scales, inverse,
              head_max, head_peer, head_inverse,
              load_sem, head_load, rs_send, rs_recv, ag_send, ag_recv, send_sem, recv_sem,
-             top_send, top_recv, head_send, head_recv, ep_send, ep_recv, row_send, row_recv, go):
+             top_send, top_recv, head_send, head_recv, ep_send, ep_recv, row_send, row_recv,
+             pair_send, pair_recv, relay_send, relay_recv, go):
     experts, rows, columns, blocks, n_ep, n_fsdp = sizes
     me, group = lax.axis_index("fsdp"), lax.axis_index("ep")
-    inner = is_inner(me, n_fsdp)
+    inner, side = is_inner(me, n_fsdp), me % 2
     last = rows - (blocks - 1) * LANES
     half = n_fsdp // 2
     lead = min(3, experts)
@@ -59,6 +60,8 @@
     starts = [expert * (n_fsdp - 1) - 2 * max(0, expert - fresh) for expert in range(experts)]
     mine = pl.ds(pl.multiple_of(me * columns, LANES), columns)
 
+    used = pl.ds(0, blocks)
+
     def rows_of(block):
         return LANES if block < blocks - 1 else last
 
@@ -111,12 +114,12 @@
 
     def max_copy(expert, step):
         owner = partner(me, step, n_fsdp)
-        return to_fsdp(local_max.at[owner, expert], peer_max.at[step, expert],
+        return to_fsdp(local_max.at[owner // 2, owner % 2, expert, used], peer_max.at[step, expert, used],
                        rs_send.at[expert, step], rs_recv.at[expert, step], owner)
 
     def scale_copy(expert, step):
         owner = partner(me, step, n_fsdp)
-        return to_fsdp(scales.at[me, expert], scales.at[me, expert],
+        return to_fsdp(scales.at[me, expert, used], scales.at[me, expert, used],
                        ag_send.at[expert, step], ag_recv.at[expert, step], owner)
 
     def head_copy(step):
@@ -187,18 +190,74 @@
         wait_loads(t, expert, turn)
         owner, slot = partner(me, turn, n_fsdp), t % SLOTS
         for block in range(1 if expert == 0 else 0, blocks):
-            local_max[owner, expert, pl.ds(block, 1), :] = tops(merged(slot, block, LANES))
+            local_max[owner // 2, owner % 2, expert, pl.ds(block, 1), :] = tops(merged(slot, block, LANES))
         load_ahead(index, turn)
 
+    def twice(start, body):
+        over(0, (n_fsdp - start) // 2, lambda turn: body(start + 2 * turn))
+
     def share_scales(expert):
-        over(1, n_fsdp, lambda step: max_copy(expert, step).wait_recv())
-        top = local_max[me, expert]
-        for step in range(1, n_fsdp):
-            top = jnp.maximum(top, peer_max[step, expert])
-        scales[me, expert] = top
+        steps = range(1, n_fsdp) if expert == 0 else range(2, n_fsdp, 2)
+        if expert == 0:
+            over(1, n_fsdp, lambda step: max_copy(expert, step).wait_recv())
+        else:
+            twice(2, lambda step: max_copy(expert, step).wait_recv())
+        top = local_max[me // 2, side, expert, used]
+        for step in steps:
+            top = jnp.maximum(top, peer_max[step, expert, used])
+        scales[me, expert, used] = top
         if expert == 0:
             scales[me, 0, pl.ds(0, 1), :] = head_max[pl.ds(me, 1), :]
-        over(1, n_fsdp, lambda step: scale_copy(expert, step).start())
+            over(1, n_fsdp, lambda step: scale_copy(expert, step).start())
+        else:
+            scale_copy(expert, 1).start()
+            twice(2, lambda step: scale_copy(expert, step).start())
+
+    def pair_copy(expert):
+        return to_fsdp(local_max.at[:, 1 - side, expert, used], pair_max.at[:, expert, used],
+                       pair_send.at[expert], pair_recv.at[expert], partner(me, 1, n_fsdp))
+
+    def relay_copy(expert, step):
+        source = partner(me, step, n_fsdp)
+        return to_fsdp(scales.at[source, expert, used], scales.at[source, expert, used],
+                       relay_send.at[expert, step], relay_recv.at[expert, step], partner(me, 1, n_fsdp))
+
+    def start_max(expert):
+        if expert == 0:
+            over(1, n_fsdp, lambda step: max_copy(expert, step).start())
+        else:
+            pair_copy(expert).start()
+
+    def join_pair(expert):
+        if expert:
+            pair_copy(expert).wait_recv()
+            for place in range(half):
+                local_max[place, side, expert, used] = jnp.maximum(
+                    local_max[place, side, expert, used], pair_max[place, expert, used])
+            twice(2, lambda step: max_copy(expert, step).start())
+
+    def relay(expert):
+        if expert == 0:
+            over(1, n_fsdp, lambda step: scale_copy(expert, step).wait_recv())
+        else:
+            def pass_on(step):
+                scale_copy(expert, step).wait_recv()
+                relay_copy(expert, step).start()
+
+            twice(2, pass_on)
+            scale_copy(expert, 1).wait_recv()
+
+    def settle(expert):
+        if expert:
+            twice(2, lambda step: relay_copy(expert, step).wait_recv())
+
+    stages, reached = (start_max, join_pair, share_scales, relay, settle), [0] * experts
+
+    def reach(expert, stage):
+        if expert < experts:
+            while reached[expert] < stage:
+                stages[reached[expert]](expert)
+                reached[expert] += 1
 
     def spread(row):
         return jnp.broadcast_to(row, (LANES, LANES)).T
@@ -265,12 +324,12 @@
                 over(half, n_fsdp, functools.partial(find_max, index, expert))
             else:
                 over(0, n_fsdp, functools.partial(find_max, index, expert))
-                share_scales(expert - 1)
-            over(1, n_fsdp, lambda step: max_copy(expert, step).start())
+                reach(expert - 1, 3 if expert == 1 else 2)
+            reach(expert, 1)
+            if index >= lead:
+                reach(expert, 2)
             if expert == 0:
                 over(half + half // 2, n_fsdp - 1, scale_head)
-                if lead == 1:
-                    share_scales(0)
             if expert == min(1, lead - 1):
                 over(n_fsdp - 1, n_fsdp, scale_head)
                 over(1, half, scale_head)
@@ -278,23 +337,36 @@
                 over(1, n_fsdp, lambda step: row_copy(step).wait())
                 over(1, n_ep, lambda step: column_copy(step).start())
         else:
-            if lead > 1 and expert == experts - lead + 1:
-                share_scales(experts - 1)
-            over(1, n_fsdp, lambda step: scale_copy(expert, step).wait_recv())
+            reach(expert, 5)
             inverse[...] = 1.0 / scales[:, expert]
             zero = (n_fsdp - turns[index]) % n_fsdp
             stop = n_fsdp - 2 if expert >= fresh else n_fsdp
-            over(0, zero, functools.partial(scale_piece, index, expert, "sent"))
+            if expert == 0 and zero:
+                over(0, 1, functools.partial(scale_piece, index, expert, "sent"))
+                reach(1, 3)
+                reach(2, 2)
+                over(1, zero, functools.partial(scale_piece, index, expert, "sent"))
+            else:
+                over(0, zero, functools.partial(scale_piece, index, expert, "sent"))
             scale_piece(index, expert, "own", zero)
             over(zero + 1, stop, functools.partial(scale_piece, index, expert, "sent"))
             over(stop, n_fsdp, functools.partial(scale_piece, index, expert, "late"))
+            reach(expert + 1, 4)
+            reach(expert + 2, 3)
 
     scales_out[...] = scales[me]
     over(1, n_ep, lambda step: column_copy(step).wait())
     over(1, n_fsdp, lambda step: head_copy(step).wait())
     for expert in range(experts):
-        over(1, n_fsdp, lambda step: max_copy(expert, step).wait_send())
-        over(1, n_fsdp, lambda step: scale_copy(expert, step).wait_send())
+        if expert == 0:
+            over(1, n_fsdp, lambda step: max_copy(expert, step).wait_send())
+            over(1, n_fsdp, lambda step: scale_copy(expert, step).wait_send())
+        else:
+            pair_copy(expert).wait_send()
+            scale_copy(expert, 1).wait_send()
+            twice(2, lambda step: max_copy(expert, step).wait_send())
+            twice(2, lambda step: scale_copy(expert, step).wait_send())
+            twice(2, lambda step: relay_copy(expert, step).wait_send())
         over(1, n_fsdp if expert < fresh else n_fsdp - 2, lambda step: piece_copy(expert, step).wait())
     if fresh < experts:
         @pl.when(inner)
@@ -407,7 +479,8 @@
                 pltpu.VMEM((n_fsdp, LANES, columns), jnp.float32),
                 pltpu.VMEM((n_fsdp, LANES, columns), jnp.bfloat16),
                 pltpu.VMEM((experts * (n_fsdp - 1) - 2 * n_late, rows, columns), jnp.bfloat16),
-                pltpu.VMEM((n_fsdp, experts, held, LANES), jnp.float32),
+                pltpu.VMEM((n_fsdp // 2, 2, experts, held, LANES), jnp.float32),
+                pltpu.VMEM((n_fsdp // 2, experts, held, LANES), jnp.float32),
                 pltpu.VMEM((n_fsdp, experts, held, LANES), jnp.float32),
                 pltpu.VMEM((n_fsdp, experts, held, LANES), jnp.float32),
                 pltpu.VMEM((n_fsdp, held, LANES), jnp.float32),
@@ -420,10 +493,11 @@
                 dma((experts, n_fsdp)), dma((experts, n_fsdp)),
                 dma((n_fsdp,)), dma((n_fsdp,)), dma((n_fsdp,)), dma((n_fsdp,)),
                 dma((n_ep,)), dma((n_ep,)), dma((n_fsdp,)), dma((n_fsdp,)),
+                dma((experts,)), dma((experts,)), dma((experts, n_fsdp)), dma((experts, n_fsdp)),
                 pltpu.SemaphoreType.REGULAR,
             ],
             compiler_params=pltpu.CompilerParams(
-                collective_id=0, has_side_effects=True, vmem_limit_bytes=32560 * 1024),
+                collective_id=0, has_side_effects=True, vmem_limit_bytes=34 * 1024 * 1024),
         )(master_down, second_down, router_weight.T, router_gain[None, :])
         final_down, scale_down, serve_router, token = pl.pallas_call(
             functools.partial(write, (experts, rows, blocks, n_ep, n_fsdp, depth)),

time: 584 us -> 581 us (level)
    pallas_call x1, Pallas kernels: 98.6 us -> 62.8 us  [on_device(): pl.pallas_call(functools.partial(exchange_late, (experts, rows, n_fsdp)),...]
    pallas_call x1, Pallas kernels: 474 us -> 507 us  [on_device(): pl.pallas_call(functools.partial(exchange, (experts, rows, columns, block...]
where the time goes in v3:
time: 581 us
  Pallas kernels  580 us (100%)
    pallas_call x1, Pallas kernels, on_device(): pl.pallas_call(functools.partial(exchange, (experts, rows, columns, block...  507 us
    pallas_call x1, Pallas kernels, on_device(): pl.pallas_call(functools.partial(exchange_late, (experts, rows, n_fsdp)),...  62.8 us

profile of v3, /device:TPU:9, one launch (start us, length us, event | category | flops | bytes accessed | tf_op | source)
XLA Modules:
  0.0 580.6 jit_solution(6035909026823516851)
XLA Ops:
  0.6 507.0 %shard_map.67 = (bf16[4,800,4096]{2,1,0:T(8,128)(2,1)S(1)}, f32[4,8,128]{2,1,0:T(8,128)S(1)}, bf16[8,4,4,512]{3,2,1,0:T(4,128)(2,1)S(1)}, bf16[1,2,800,512]{3,2,1,0:T(8,128)(2,1)S(1)}) custom-call(f32[4,6400,512]{2,1,0:T(8,128)} %master.1, bf16[4,6400,512]{2,1,0:T(8,128)(2,1)} %second.1, f32[4,512]{1,0:T(4,128)} %bitcast.3, f32[1,512]{1,0:T(1,128)} %bitcast.4), custom_call_target="tpu_custom_call" | custom-call | tf_op jit(solution)/shard_map/pallas_call | solution.py:466
  507.7 8.9 %shard_map.68 = (bf16[4,800,4096]{2,1,0:T(8,128)(2,1)}, f32[4,800]{1,0:T(4,128)}, bf16[16,4096]{1,0:T(8,128)(2,1)}, f32[8,128]{1,0:T(8,128)S(1)}) custom-call(bf16[4,800,4096]{2,1,0:T(8,128)(2,1)S(1)} %get-tuple-element.11.pieces, f32[4,8,128]{2,1,0:T(8,128)S(1)} %get-tuple-element.12.scales, bf16[8,4,4,512]{3,2,1,0:T(4,128)(2,1)S(1)} %get-tuple-element.13.parts), custom_call_target="tpu_custom_call" | custom-call | tf_op jit(solution)/shard_map/pallas_call | solution.py:502
  516.6 62.8 %shard_map.69.tail = bf16[1,2,800,512]{3,2,1,0:T(8,128)(2,1)S(1)} custom-call(bf16[1,2,800,512]{3,2,1,0:T(8,128)(2,1)S(1)} %get-tuple-element.15.late, f32[8,128]{1,0:T(8,128)S(1)} %get-tuple-element.16.written), custom_call_target="tpu_custom_call" | custom-call | tf_op jit(solution)/shard_map/pallas_call | solution.py:521
  579.4 1.2 shard_map.70
